TPU v7x, 32 devices: a whole 2x2x4 slice. The times are simulated.
32 devices in a mesh: ulysses: 8 (over z, x), blk: 4 (over y, core).
Axes of the slice: x: 2, y: 2, z: 4, core: 2. Of those that a mesh axis runs over, the one named last changes fastest.
Arguments:
- queries: bfloat16 [4, 512, 4096], P('blk', 'ulysses'), may hold values from -6 to 6
- key_rows: bfloat16 [4, 512, 1024], P('blk', 'ulysses'), may hold values from -6 to 6
- value_rows: bfloat16 [4, 512, 1024], P('blk', 'ulysses'), may hold values from -6 to 6
- tile_segment: int32 [16], replicated, may hold values from 0 to 3, never falling along the last dimension, each value on 1 to 8 neighbouring positions
Outputs:
- attended: bfloat16 [4, 512, 4096], P('blk', 'ulysses')
Inputs may be any that keep to these rules, and one draw needn't show every extreme that they name: `tile_segment`: segment numbers never fall along the sequence and each segment covers 1 to 8 tiles.
All inputs are finite; a program needn't handle non-finite values.
Results may differ from a plain program's by a relative error of at most 0.0045.
Values may be sent and summed in bfloat16 or wider, within the bound.
A program may use at most 64 MiB of HBM per device.

v0:
```python
import math

import jax
import jax.numpy as jnp
from jax import lax
from jax.sharding import PartitionSpec as P

HEAD_DIM = 128
TILE = 128


masked_score = -1e30


def segment_of(positions, tile_segment):
    tiles_total = tile_segment.shape[0]
    matches = (positions // TILE)[:, None] == jnp.arange(tiles_total, dtype=jnp.int32)[None, :]
    return jnp.sum(jnp.where(matches, tile_segment[None, :], 0), axis=1)


def visible(query_pos, query_seg, key_pos, key_seg):
    earlier = key_pos[None, :] <= query_pos[:, None]
    same_image = (key_seg[None, :] == query_seg[:, None]) & (query_seg[:, None] % 2 == 1)
    return earlier | same_image


def widen(source_rows, groups):
    tokens_dev = source_rows.shape[1]
    heads_here = source_rows.shape[2] // HEAD_DIM
    factor = max(1, groups // heads_here)
    spread = jnp.repeat(source_rows.reshape(1, tokens_dev, heads_here, HEAD_DIM), factor, axis=2)
    return spread.reshape(1, tokens_dev, heads_here * factor * HEAD_DIM)


def same_rows(row_ids):
    return row_ids


def update(current, allowed, query_block, key_block, value_block):
    maxima, denominators, weighted = current
    scores = jnp.einsum(
        "qkgd,skd->kgqs", query_block, key_block, preferred_element_type=jnp.float32
    )
    scores = jnp.where(allowed[None, None], scores * HEAD_DIM ** (-0.5), masked_score)
    new_max = jnp.maximum(maxima, jnp.max(scores, axis=3))
    weights = jnp.where(allowed[None, None], jnp.exp(scores - new_max[..., None]), 0.0)
    factor = jnp.exp(maxima - new_max)
    denominators = factor * denominators + jnp.sum(weights, axis=3)
    product = jnp.einsum(
        "kgqs,skd->kgqd",
        weights.astype(jnp.bfloat16),
        value_block,
        preferred_element_type=jnp.float32,
    )
    weighted = factor[..., None] * weighted + product
    return (new_max, denominators, weighted)


def keep_state(current, allowed, query_block, key_block, value_block):
    return current


def build_fold(query_rows, query_pos, tile_segment, key_position, kv_width):
    rows_total = query_rows.shape[0]
    kv_local = kv_width // HEAD_DIM
    group_size = query_rows.shape[1] // HEAD_DIM // kv_local
    shaped = query_rows.reshape(rows_total, kv_local, group_size, HEAD_DIM)
    query_seg = segment_of(query_pos, tile_segment)
    half_rows = rows_total // 2

    def fold_step(running, portion, offset):
        key_part, value_part = portion
        portion_rows = key_part.shape[0]
        block_rows = math.gcd(portion_rows, 512)
        block_total = portion_rows // block_rows
        key_blocks = key_part.reshape(block_total, block_rows, kv_local, HEAD_DIM)
        value_blocks = value_part.reshape(block_total, block_rows, kv_local, HEAD_DIM)

        def one_block(halves, inputs):
            key_block, value_block, block_number = inputs
            key_pos = key_position(
                block_number * block_rows + jnp.arange(block_rows, dtype=jnp.int32)
            )
            key_seg = segment_of(key_pos, tile_segment)
            results = []
            for half_index in range(2):
                row_low = half_index * half_rows
                row_high = row_low + half_rows
                allowed = visible(
                    query_pos[row_low:row_high], query_seg[row_low:row_high], key_pos, key_seg
                )
                results.append(
                    lax.cond(
                        jnp.any(allowed),
                        update,
                        keep_state,
                        halves[half_index],
                        allowed,
                        shaped[row_low:row_high],
                        key_block,
                        value_block,
                    )
                )
            return ((results[0], results[1]), None)

        running, unused = lax.scan(
            one_block, running, (key_blocks, value_blocks, jnp.arange(block_total, dtype=jnp.int32))
        )
        return running

    def empty_half():
        return (
            jnp.full((kv_local, group_size, half_rows), masked_score, jnp.float32),
            jnp.zeros((kv_local, group_size, half_rows), jnp.float32),
            jnp.zeros((kv_local, group_size, half_rows, HEAD_DIM), jnp.float32),
        )

    return (fold_step, (empty_half(), empty_half()))


def finish(running):
    outputs = [weighted / denominators[..., None] for maxima, denominators, weighted in running]
    joined = jnp.concatenate(outputs, axis=2)
    kv_local, group_size, rows_total, head_dim = joined.shape
    joined = jnp.transpose(joined, (2, 0, 1, 3)).reshape(
        rows_total, kv_local * group_size * head_dim
    )
    return joined.astype(jnp.bfloat16)


def local(queries, key_rows, value_rows, tile_segment):
    ulysses_count = lax.axis_size("ulysses")
    tokens_dev = queries.shape[1]
    block_len = tokens_dev * ulysses_count
    block_index = lax.axis_index("blk")
    local_rows = jnp.arange(block_len, dtype=jnp.int32)
    moved = (
        lax.all_to_all(queries, "ulysses", split_axis=2, concat_axis=1, tiled=True),
        lax.all_to_all(
            widen(key_rows, ulysses_count), "ulysses", split_axis=2, concat_axis=1, tiled=True
        ),
        lax.all_to_all(
            widen(value_rows, ulysses_count), "ulysses", split_axis=2, concat_axis=1, tiled=True
        ),
    )
    query_rows, key_local, value_local = (moved[0][0], moved[1][0], moved[2][0])
    query_pos = block_index * block_len + local_rows
    fold_step, initial = build_fold(
        query_rows, query_pos, tile_segment, same_rows, key_local.shape[1]
    )
    running = fold_step(
        initial,
        (
            lax.all_gather(key_local, "blk", axis=0, tiled=True),
            lax.all_gather(value_local, "blk", axis=0, tiled=True),
        ),
        jnp.int32(0),
    )
    attended = lax.all_to_all(
        finish(running)[None], "ulysses", split_axis=1, concat_axis=2, tiled=True
    )
    return attended


def solution(mesh):
    return jax.shard_map(
        local,
        mesh=mesh,
        in_specs=(
            P("blk", "ulysses", None),
            P("blk", "ulysses", None),
            P("blk", "ulysses", None),
            P(),
        ),
        out_specs=P("blk", "ulysses", None),
        check_vma=False,
    )
```

profile of v0, /device:TPU:5, one launch (start us, length us, event | category | flops | bytes accessed | tf_op | source)
XLA Modules:
  0.0 137.4 jit_solution(7677934682182908862)
XLA Ops:
  0.0 1.3 copy.59
  1.3 0.6 broadcast.215
  1.9 2.3 %reduce.4 = bf16[1024,64]{1,0:T(8,128)(2,1)S(1)} reduce(bf16[1024,1,64]{2,1,0:T(2,128)(2,1)S(1)} %bitcast.162, bf16[]{:T(256)} %broadcast.215), dimensions={1}, to_apply=%bitcast.126.reduce_sub_computation | reduce | bytes 262146
  4.2 0.9 reshape.154
  5.1 5.5 %all-to-all-start = ((bf16[8,2,4096]{2,1,0:T(2,128)(2,1)}), bf16[8,2,4096]{2,1,0:T(2,128)(2,1)S(1)}, u32[]{:S(2)}, u32[]{:S(2)}) async-start(bf16[8,2,4096]{2,1,0:T(2,128)(2,1)} %reshape.154), calls=%async_computation | async-start | bytes 262144 | tf_op jit(solution)/shard_map/all_to_all | solution.py:139
  11.0 2.3 %reduce.5 = bf16[1024,64]{1,0:T(8,128)(2,1)S(1)} reduce(bf16[1024,1,64]{2,1,0:T(2,128)(2,1)S(1)} %bitcast.163, bf16[]{:T(256)} %broadcast.215), dimensions={1}, to_apply=%bitcast.128.reduce_sub_computation | reduce | bytes 262146
  13.3 0.9 reshape.156
  14.2 2.6 %all-to-all-done = bf16[8,2,4096]{2,1,0:T(2,128)(2,1)S(1)} async-done(((bf16[8,2,4096]{2,1,0:T(2,128)(2,1)}), bf16[8,2,4096]{2,1,0:T(2,128)(2,1)S(1)}, u32[]{:S(2)}, u32[]{:S(2)}) %all-to-all-start) | async-done | bytes 131104 | tf_op jit(solution)/shard_map/all_to_all | solution.py:139
  16.8 3.4 %all-to-all-start.1 = ((bf16[8,2,4096]{2,1,0:T(2,128)(2,1)}), bf16[8,2,4096]{2,1,0:T(2,128)(2,1)S(1)}, u32[]{:S(2)}, u32[]{:S(2)}) async-start(bf16[8,2,4096]{2,1,0:T(2,128)(2,1)} %reshape.156), calls=%async_computation.1 | async-start | bytes 262144 | tf_op jit(solution)/shard_map/all_to_all | solution.py:142
  20.2 2.8 %copy.65 = bf16[1,64,4096]{1,0,2:T(2,128)(2,1)S(1)} copy(bf16[1,64,4096]{2,1,0:T(8,128)(2,1)S(1)} %copy-done) | data formatting | bytes 1048576 | tf_op args[0]
  23.0 22.5 %reduce.6 = bf16[4096,64]{1,0:T(8,128)(2,1)S(1)} reduce(bf16[4096,1,64]{2,1,0:T(2,128)(2,1)S(1)} %bitcast.152, bf16[]{:T(256)} %broadcast.215), dimensions={1}, to_apply=%bitcast.130.reduce_sub_computation | reduce | bytes 1048578
  45.5 1.5 %reshape.158 = bf16[8,2,16384]{2,1,0:T(2,128)(2,1)} reshape(bf16[4096,64]{1,0:T(8,128)(2,1)S(1)} %reduce.6) | data formatting | bytes 1048576
  47.1 5.3 %all-to-all-start.2 = ((bf16[8,2,16384]{2,1,0:T(2,128)(2,1)}), bf16[8,2,16384]{2,1,0:T(2,128)(2,1)}, u32[]{:S(2)}, u32[]{:S(2)}) async-start(bf16[8,2,16384]{2,1,0:T(2,128)(2,1)} %reshape.158), calls=%async_computation.2 | async-start | bytes 1048576 | tf_op jit(solution)/shard_map/all_to_all | solution.py:138
  53.9 9.2 %all_gather.6 = bf16[2048,128]{1,0:T(8,128)(2,1)S(1)} all-gather(bf16[512,128]{1,0:T(8,128)(2,1)S(1)} %bitcast.169), channel_id=1, replica_groups=mesh['ulysses'=8,'blk'=4] {'blk'}, dimensions={0}, use_global_device_ids=true | all-gather | bytes 655360 | tf_op jit(solution)/shard_map/all_gather | solution.py:154
  63.1 7.3 %all_gather.7 = bf16[2048,128]{1,0:T(8,128)(2,1)S(1)} all-gather(bf16[512,128]{1,0:T(8,128)(2,1)S(1)} %bitcast.170), channel_id=1, replica_groups=mesh['ulysses'=8,'blk'=4] {'blk'}, dimensions={0}, use_global_device_ids=true | all-gather | bytes 655360 | tf_op jit(solution)/shard_map/all_gather | solution.py:155
  70.4 4.1 %reshape.159 = bf16[4096,1,64]{2,1,0:T(2,128)(2,1)S(1)} reshape(bf16[8,2,16384]{2,1,0:T(2,128)(2,1)} %all-to-all-done.2) | data formatting | bytes 1048576
  74.5 3.6 %copy.66 = bf16[1,64,4096]{2,1,0:T(8,128)(2,1)} copy(bf16[1,64,4096]{1,0,2:T(2,128)(2,1)S(1)} %bitcast.151) | data formatting | bytes 1048576 | tf_op jit(solution)/shard_map/all_to_all | solution.py:138
  78.1 1.2 copy.81
  79.9 31.0 %while.23 = (s32[]{:T(128)}, f32[1,4,256]{2,1,0:T(4,128)S(1)}, f32[1,4,256]{2,1,0:T(4,128)S(1)}, f32[1,4,256,128]{3,2,1,0:T(8,128)S(1)}, f32[1,4,256]{2,1,0:T(4,...) while((s32[]{:T(128)}, f32[1,4,256]{2,1,0:T(4,128)S(1)}, ...), condition=%wide.region_13.14_spmd, body=%wide.region_1.13_spmd.sunk | while | flops 552381440 | bytes 17462768 | solution.py:106
  79.9 0.6 dynamic_slice.28
  81.3 1.1 fusion.59
  83.0 1.9 %conditional.5 = ((f32[1,4,256]{2,1,0:T(4,128)S(1)}, f32[1,4,256]{2,1,0:T(4,128)S(1)}, f32[1,4,256,128]{3,2,1,0:T(8,128)S(1)})) conditional(s32[]{:T(128)} %convert_element_type.47, (f32[1,4,256]{2,1,0:T(4,128)S(1)}, f32[1,4,256]{2,1,0:T(4,128)S(1)}, f32[1,4,256,128]{3,2,1,0:T(8,128)S(1)}) %tuple.82, (pred[256,512]{0,1:T(8,128)(4,1)S(1)}, ...), branch_computations={%region_9.9_spmd, %region_10.12_spmd} | conditional | flops 275516416 | bytes 8323104 | solution.py:93
  83.1 0.5 fusion.20
  83.5 0.5 fusion.22
  84.1 0.9 fusion.23
  85.7 2.0 %conditional.4 = ((f32[1,4,256]{2,1,0:T(4,128)S(1)}, f32[1,4,256]{2,1,0:T(4,128)S(1)}, f32[1,4,256,128]{3,2,1,0:T(8,128)S(1)})) conditional(s32[]{:T(128)} %convert_element_type.46, (f32[1,4,256]{2,1,0:T(4,128)S(1)}, f32[1,4,256]{2,1,0:T(4,128)S(1)}, f32[1,4,256,128]{3,2,1,0:T(8,128)S(1)}) %tuple.80, (pred[256,512]{0,1:T(8,128)(4,1)S(1)}, ...), branch_computations={%region_4.4_spmd, %region_5.7_spmd} | conditional | flops 275516416 | bytes 8323104 | solution.py:93
  85.7 0.5 fusion
  86.2 0.5 fusion.2
  86.8 0.9 fusion.3
  87.7 0.6 dynamic_slice.28
  89.0 1.1 fusion.59
  90.8 2.0 %conditional.5 = ((f32[1,4,256]{2,1,0:T(4,128)S(1)}, f32[1,4,256]{2,1,0:T(4,128)S(1)}, f32[1,4,256,128]{3,2,1,0:T(8,128)S(1)})) conditional(s32[]{:T(128)} %convert_element_type.47, (f32[1,4,256]{2,1,0:T(4,128)S(1)}, f32[1,4,256]{2,1,0:T(4,128)S(1)}, f32[1,4,256,128]{3,2,1,0:T(8,128)S(1)}) %tuple.82, (pred[256,512]{0,1:T(8,128)(4,1)S(1)}, ...), branch_computations={%region_9.9_spmd, %region_10.12_spmd} | conditional | flops 275516416 | bytes 8323104 | solution.py:93
  90.8 0.5 fusion.20
  91.3 0.5 fusion.22
  91.9 0.9 fusion.23
  93.4 2.0 %conditional.4 = ((f32[1,4,256]{2,1,0:T(4,128)S(1)}, f32[1,4,256]{2,1,0:T(4,128)S(1)}, f32[1,4,256,128]{3,2,1,0:T(8,128)S(1)})) conditional(s32[]{:T(128)} %convert_element_type.46, (f32[1,4,256]{2,1,0:T(4,128)S(1)}, f32[1,4,256]{2,1,0:T(4,128)S(1)}, f32[1,4,256,128]{3,2,1,0:T(8,128)S(1)}) %tuple.80, (pred[256,512]{0,1:T(8,128)(4,1)S(1)}, ...), branch_computations={%region_4.4_spmd, %region_5.7_spmd} | conditional | flops 275516416 | bytes 8323104 | solution.py:93
  93.5 0.5 fusion
  94.0 0.5 fusion.2
  94.5 0.9 fusion.3
  95.4 0.6 dynamic_slice.28
  96.8 1.1 fusion.59
  98.5 2.0 %conditional.5 = ((f32[1,4,256]{2,1,0:T(4,128)S(1)}, f32[1,4,256]{2,1,0:T(4,128)S(1)}, f32[1,4,256,128]{3,2,1,0:T(8,128)S(1)})) conditional(s32[]{:T(128)} %convert_element_type.47, (f32[1,4,256]{2,1,0:T(4,128)S(1)}, f32[1,4,256]{2,1,0:T(4,128)S(1)}, f32[1,4,256,128]{3,2,1,0:T(8,128)S(1)}) %tuple.82, (pred[256,512]{0,1:T(8,128)(4,1)S(1)}, ...), branch_computations={%region_9.9_spmd, %region_10.12_spmd} | conditional | flops 275516416 | bytes 8323104 | solution.py:93
  98.6 0.5 fusion.20
  99.1 0.5 fusion.22
  99.6 0.9 fusion.23
  101.2 2.0 %conditional.4 = ((f32[1,4,256]{2,1,0:T(4,128)S(1)}, f32[1,4,256]{2,1,0:T(4,128)S(1)}, f32[1,4,256,128]{3,2,1,0:T(8,128)S(1)})) conditional(s32[]{:T(128)} %convert_element_type.46, (f32[1,4,256]{2,1,0:T(4,128)S(1)}, f32[1,4,256]{2,1,0:T(4,128)S(1)}, f32[1,4,256,128]{3,2,1,0:T(8,128)S(1)}) %tuple.80, (pred[256,512]{0,1:T(8,128)(4,1)S(1)}, ...), branch_computations={%region_4.4_spmd, %region_5.7_spmd} | conditional | flops 275516416 | bytes 8323104 | solution.py:93
  101.2 0.5 fusion
  101.7 0.5 fusion.2
  102.3 0.9 fusion.3
  103.2 0.6 dynamic_slice.28
  104.5 1.1 fusion.59
  106.3 2.0 %conditional.5 = ((f32[1,4,256]{2,1,0:T(4,128)S(1)}, f32[1,4,256]{2,1,0:T(4,128)S(1)}, f32[1,4,256,128]{3,2,1,0:T(8,128)S(1)})) conditional(s32[]{:T(128)} %convert_element_type.47, (f32[1,4,256]{2,1,0:T(4,128)S(1)}, f32[1,4,256]{2,1,0:T(4,128)S(1)}, f32[1,4,256,128]{3,2,1,0:T(8,128)S(1)}) %tuple.82, (pred[256,512]{0,1:T(8,128)(4,1)S(1)}, ...), branch_computations={%region_9.9_spmd, %region_10.12_spmd} | conditional | flops 275516416 | bytes 8323104 | solution.py:93
  106.3 0.5 fusion.20
  106.8 0.5 fusion.22
  107.4 0.9 fusion.23
  108.9 2.0 %conditional.4 = ((f32[1,4,256]{2,1,0:T(4,128)S(1)}, f32[1,4,256]{2,1,0:T(4,128)S(1)}, f32[1,4,256,128]{3,2,1,0:T(8,128)S(1)})) conditional(s32[]{:T(128)} %convert_element_type.46, (f32[1,4,256]{2,1,0:T(4,128)S(1)}, f32[1,4,256]{2,1,0:T(4,128)S(1)}, f32[1,4,256,128]{3,2,1,0:T(8,128)S(1)}) %tuple.80, (pred[256,512]{0,1:T(8,128)(4,1)S(1)}, ...), branch_computations={%region_4.4_spmd, %region_5.7_spmd} | conditional | flops 275516416 | bytes 8323104 | solution.py:93
  109.0 0.5 fusion
  109.5 0.5 fusion.2
  110.0 0.9 fusion.3
  111.5 0.9 copy.73
  112.4 3.9 %reduce.7 = bf16[512,512]{1,0:T(8,128)(2,1)S(1)} reduce(bf16[512,1,512]{2,1,0:T(2,128)(2,1)S(1)} %bitcast.154, bf16[]{:T(256)} %broadcast.215), dimensions={1}, to_apply=%bitcast.132.reduce_sub_computation | reduce | bytes 1048578
  116.6 19.2 %all_to_all.63 = bf16[8,2,16384]{2,1,0:T(2,128)(2,1)S(1)} all-to-all(bf16[8,2,16384]{2,1,0:T(2,128)(2,1)S(1)} %reshape.160), channel_id=1, replica_groups=mesh['ulysses'=8,'blk'=4] {'ulysses'}, dimensions={0} | all-to-all | bytes 1048576 | tf_op jit(solution)/shard_map/all_to_all | solution.py:159
  135.9 0.5 reshape.161
  136.5 0.8 copy.78
  (84 shorter events, 4.2 us)
Async XLA Ops:
  0.0 10.6 %copy-start.1 = (bf16[1,64,1024]{2,1,0:T(8,128)(2,1)S(1)}, bf16[1,64,1024]{2,1,0:T(8,128)(2,1)}, u32[]{:S(2)}) copy-start(bf16[1,64,1024]{2,1,0:T(8,128)(2,1)} %param.12) | copy-start | bytes 393220
  0.0 20.2 %copy-start = (bf16[1,64,4096]{2,1,0:T(8,128)(2,1)S(1)}, bf16[1,64,4096]{2,1,0:T(8,128)(2,1)}, u32[]{:S(2)}) copy-start(bf16[1,64,4096]{2,1,0:T(8,128)(2,1)} %param.10) | copy-start | bytes 1572868
  5.1 11.7 %all-to-all-start = ((bf16[8,2,4096]{2,1,0:T(2,128)(2,1)}), bf16[8,2,4096]{2,1,0:T(2,128)(2,1)S(1)}, u32[]{:S(2)}, u32[]{:S(2)}) async-start(bf16[8,2,4096]{2,1,0:T(2,128)(2,1)} %reshape.154), calls=%async_computation | async-start | bytes 262144 | tf_op jit(solution)/shard_map/all_to_all | solution.py:139
  16.8 30.3 %all-to-all-start.1 = ((bf16[8,2,4096]{2,1,0:T(2,128)(2,1)}), bf16[8,2,4096]{2,1,0:T(2,128)(2,1)S(1)}, u32[]{:S(2)}, u32[]{:S(2)}) async-start(bf16[8,2,4096]{2,1,0:T(2,128)(2,1)} %reshape.156), calls=%async_computation.1 | async-start | bytes 262144 | tf_op jit(solution)/shard_map/all_to_all | solution.py:142
  23.0 24.0 %copy-start.2 = (s32[16]{0:T(128)S(1)}, s32[16]{0:T(128)}, u32[]{:S(2)}) copy-start(s32[16]{0:T(128)} %param.13) | copy-start | bytes 196
  47.1 23.3 %all-to-all-start.2 = ((bf16[8,2,16384]{2,1,0:T(2,128)(2,1)}), bf16[8,2,16384]{2,1,0:T(2,128)(2,1)}, u32[]{:S(2)}, u32[]{:S(2)}) async-start(bf16[8,2,16384]{2,1,0:T(2,128)(2,1)} %reshape.158), calls=%async_computation.2 | async-start | bytes 1048576 | tf_op jit(solution)/shard_map/all_to_all | solution.py:138
where the time goes:
time: 138 us; the launch traced here: 137 us
  other arithmetic  40.5 us (29%)
  blocking collectives  35.7 us (26%)
  local copies, waits for them, and re-layouts  24.7 us (18%)
  starting transfers between devices  14.2 us (10%)
  matrix products  10.8 us (8%)
  loops' own time  8.49 us (6%)
  waiting for transfers between devices  2.59 us (2%)
    unnamed x4, other arithmetic  31 us
    all_to_all x1, blocking collectives, local(): lax.all_to_all(finish(running)[None], 'ulysses', split_axis=1, concat_axi...  19.2 us
    unnamed x22, local copies, waits for them, and re-layouts  15.4 us
    all_gather x1, blocking collectives, local(): lax.all_gather(key_local, 'blk', axis=0, tiled=True)  9.19 us
    another operation x1, loops' own time, fold_step(): lax.scan(one_block, running, (key_blocks, value_blocks, jnp.arange(block_...  8.16 us
    all_gather x1, blocking collectives, local(): lax.all_gather(value_local, 'blk', axis=0, tiled=True)  7.26 us
    dot_general x8, matrix products, update(): jnp.einsum('kgqs,skd->kgqd', weights.astype(jnp.bfloat16), value_block, p...  6.93 us
    all_to_all x1, starting transfers between devices, local(): lax.all_to_all(widen(key_rows, ulysses_count), 'ulysses', split_axis=2, c...  5.53 us
  transfers between devices with their start and end apart: 3, of which 1 were waited for; matrix products, arithmetic and copies ran while one was open for 23% of the time, Pallas kernels for 0%

commit v1 on v0

v1 whole, which is shorter than its diff:
```python
import functools
import math

import jax
import jax.numpy as jnp
from jax import lax
from jax.experimental import pallas as pl
from jax.experimental.pallas import tpu as pltpu
from jax.sharding import PartitionSpec as P

HEAD_DIM = 128
TILE = 128
MASKED = -1e30
MESH = pl.DeviceIdType.MESH


def kernel(
    dims, q_ref, k_ref, v_ref, seg_ref, out_ref,
    kv, qb, ob, m_ref, acc_ref,
    kv_recv, kv_send, chain_send, q_recv, q_send, o_recv, o_send,
):
    ulysses, blocks, hx, hb = dims
    peers = hx * hb
    gu_n, gb_n = ulysses // hx, blocks // hb
    planes = gu_n * gb_n
    rows = q_ref.shape[1]
    width = q_ref.shape[2] // peers
    group = width // HEAD_DIM
    block_len = rows * ulysses
    tile_rows = rows * hx
    scale = HEAD_DIM ** -0.5 * math.log2(math.e)

    u, b = lax.axis_index("ulysses"), lax.axis_index("blk")
    gu, gb = u // hx, b // hb
    g = gb * gu_n + gu
    me = (b % hb) * hx + u % hx

    def peer_id(p):
        return (gu * hx + p % hx, gb * hb + p // hx)

    def plane_id(other):
        return ((other % gu_n) * hx + u % hx, (other // gu_n) * hb + b % hb)

    barrier = pltpu.get_barrier_semaphore()
    for j in range(1, peers):
        pl.semaphore_signal(
            barrier, inc=1, device_id=peer_id((me + j) % peers), device_id_type=MESH
        )

    @pl.when(g > 0)
    def _():
        pl.semaphore_signal(barrier, inc=1, device_id=plane_id(g - 1), device_id_type=MESH)

    @pl.when(g < planes - 1)
    def _():
        pl.semaphore_signal(barrier, inc=1, device_id=plane_id(g + 1), device_id_type=MESH)

    ends = jnp.where(g > 0, 1, 0) + jnp.where(g < planes - 1, 1, 0)
    pl.semaphore_wait(barrier, peers - 1 + ends)

    def columns(p, wide):
        return pl.ds(pl.multiple_of(p * wide, wide), wide)

    def remote(src, dst, send, recv, device):
        return pltpu.make_async_remote_copy(
            src_ref=src, dst_ref=dst, send_sem=send, recv_sem=recv,
            device_id=device, device_id_type=MESH,
        )

    for j in range(1, peers):
        p = (me + j) % peers
        for part, source in enumerate((k_ref, v_ref)):
            remote(
                source.at[0, :, columns(p, HEAD_DIM)], kv.at[g, me, part],
                kv_send.at[j], kv_recv.at[g, me], peer_id(p),
            ).start()

    def pass_own(target, send):
        for part, source in enumerate((k_ref, v_ref)):
            remote(
                source.at[0, :, columns(me, HEAD_DIM)], kv.at[g, me, part],
                send, kv_recv.at[g, me], plane_id(target),
            ).start()

    def pass_on(slot, piece, target, send):
        remote(
            kv.at[slot, piece], kv.at[slot, piece],
            send, kv_recv.at[slot, piece], plane_id(target),
        ).start()

    @pl.when(g > 0)
    def _():
        pass_own(g - 1, chain_send.at[planes])

    @pl.when(g < planes - 1)
    def _():
        pass_own(g + 1, chain_send.at[g])

    for j in range(1, peers):
        p = (me + j) % peers
        remote(
            q_ref.at[0, :, columns(p, width)], qb.at[me],
            q_send.at[j], q_recv.at[me], peer_id(p),
        ).start()

    kv[g, me, 0] = k_ref[0, :, columns(me, HEAD_DIM)]
    kv[g, me, 1] = v_ref[0, :, columns(me, HEAD_DIM)]
    qb[me] = q_ref[0, :, columns(me, width)]
    m_ref[...] = jnp.full_like(m_ref, MASKED)
    acc_ref[...] = jnp.zeros_like(acc_ref)

    def arrived(ref, sem):
        pltpu.make_async_copy(ref, ref, sem).wait()

    for j in range(1, peers):
        p = (me + peers - j) % peers
        arrived(kv.at[g, p], kv_recv.at[g, p])

        @pl.when(g > 0)
        def _():
            pass_on(g, p, g - 1, chain_send.at[planes])

        @pl.when(g < planes - 1)
        def _():
            pass_on(g, p, g + 1, chain_send.at[g])

    for j in range(1, peers):
        p = (me + peers - j) % peers
        arrived(qb.at[p], q_recv.at[p])

    def first_position(plane, bb):
        return (plane // gu_n * hb + bb) * block_len + (plane % gu_n) * tile_rows

    delta = lax.broadcasted_iota(jnp.int32, (tile_rows, tile_rows), 1) - lax.broadcasted_iota(
        jnp.int32, (tile_rows, tile_rows), 0
    )

    def attend(slot, bb):
        query_first = first_position(g, bb)
        query_seg = seg_ref[query_first // TILE]
        keys = kv[slot, :, 0].reshape(hb * tile_rows, HEAD_DIM)
        values = kv[slot, :, 1].reshape(hb * tile_rows, HEAD_DIM)
        values = jnp.concatenate([values, jnp.ones_like(values)], axis=1)
        visible = []
        for kb in range(hb):
            key_first = first_position(slot, kb)
            key_seg = seg_ref[key_first // TILE]
            same = jnp.logical_and(key_seg == query_seg, query_seg % 2 == 1)
            limit = jnp.where(same, jnp.int32(2 ** 30), query_first - key_first)
            visible.append(delta <= limit)
        for head in range(group):
            query = qb[pl.ds(bb * hx, hx), :, head * HEAD_DIM:(head + 1) * HEAD_DIM]
            query = query.reshape(tile_rows, HEAD_DIM)
            scores = lax.dot_general(
                query, keys, (((1,), (1,)), ((), ())), preferred_element_type=jnp.float32
            )
            scores = jnp.concatenate(
                [
                    jnp.where(visible[kb], scores[:, kb * tile_rows:(kb + 1) * tile_rows], MASKED)
                    for kb in range(hb)
                ],
                axis=1,
            )
            old = m_ref[bb, head]
            new = jnp.maximum(old, jnp.max(scores, axis=1, keepdims=True))
            m_ref[bb, head] = new
            factor = jnp.exp2((old - new) * scale)
            weights = jnp.exp2((scores - new[:, :1]) * scale).astype(jnp.bfloat16)
            product = jnp.dot(weights, values, preferred_element_type=jnp.float32)
            acc_ref[bb, head] = (
                jnp.concatenate([factor, factor], axis=1) * acc_ref[bb, head] + product
            )

    def attend_all(slot):
        def one(bb, carry):
            attend(slot, bb)
            return carry

        lax.fori_loop(0, hb, one, 0)

    attend_all(g)

    near = jnp.minimum(g, planes - 1 - g)

    def step(t, carry):
        both = t <= 2 * near
        distance = jnp.where(both, (t + 1) // 2, t - near)
        below = jnp.where(both, t % 2 == 1, g > planes - 1 - g)
        slot = jnp.where(below, g - distance, g + distance)
        target = jnp.where(below, g + 1, g - 1)
        onward = jnp.logical_and(target >= 0, target < planes)
        for p in range(peers):
            arrived(kv.at[slot, p], kv_recv.at[slot, p])

            @pl.when(onward)
            def _():
                pass_on(slot, p, target, chain_send.at[slot])

        attend_all(slot)
        return carry

    lax.fori_loop(1, planes, step, 0)

    for bb in range(hb):
        for head in range(group):
            total = acc_ref[bb, head]
            ob[bb * hx:(bb + 1) * hx, :, head * HEAD_DIM:(head + 1) * HEAD_DIM] = (
                (total[:, :HEAD_DIM] / total[:, HEAD_DIM:])
                .astype(jnp.bfloat16)
                .reshape(hx, rows, HEAD_DIM)
            )
        for ux in range(hx):
            p = bb * hx + ux

            @pl.when(p != me)
            def _():
                remote(
                    ob.at[p], out_ref.at[0, :, columns(me, width)],
                    o_send.at[p], o_recv.at[me], peer_id(p),
                ).start()

    out_ref[0, :, columns(me, width)] = ob[me]
    for j in range(1, peers):
        p = (me + peers - j) % peers
        mine = out_ref.at[0, :, columns(p, width)]
        arrived(mine, o_recv.at[p])
    for j in range(1, peers):
        p = (me + j) % peers
        arrived(kv.at[g, p], kv_send.at[j])
        arrived(qb.at[p], q_send.at[j])
        arrived(ob.at[p], o_send.at[p])

    @pl.when(g > 0)
    def _():
        arrived(kv.at[g], chain_send.at[planes])

    @pl.when(g < planes - 1)
    def _():
        arrived(kv.at[g], chain_send.at[g])

    def drain(slot, carry):
        passed = jnp.logical_or(
            jnp.logical_and(slot < g, g < planes - 1), jnp.logical_and(slot > g, g > 0)
        )

        @pl.when(passed)
        def _():
            arrived(kv.at[slot], chain_send.at[slot])

        return carry

    lax.fori_loop(0, planes, drain, 0)


def local(queries, key_rows, value_rows, tile_segment):
    ulysses, blocks = lax.axis_size("ulysses"), lax.axis_size("blk")
    kv_heads = key_rows.shape[2] // HEAD_DIM
    rows = queries.shape[1]
    hb = math.gcd(blocks, max(1, kv_heads // 2))
    hx = kv_heads // hb
    planes = ulysses * blocks // kv_heads
    group = queries.shape[2] // HEAD_DIM // kv_heads
    tile_rows = hx * rows
    assert ulysses % hx == 0 and TILE % tile_rows == 0
    vmem = pl.BlockSpec(memory_space=pltpu.VMEM)
    dma = pltpu.SemaphoreType.DMA
    return pl.pallas_call(
        functools.partial(kernel, (ulysses, blocks, hx, hb)),
        out_shape=jax.ShapeDtypeStruct(queries.shape, jnp.bfloat16),
        in_specs=[vmem, vmem, vmem, pl.BlockSpec(memory_space=pltpu.SMEM)],
        out_specs=vmem,
        scratch_shapes=[
            pltpu.VMEM((planes, kv_heads, 2, rows, HEAD_DIM), jnp.bfloat16),
            pltpu.VMEM((kv_heads, rows, group * HEAD_DIM), jnp.bfloat16),
            pltpu.VMEM((kv_heads, rows, group * HEAD_DIM), jnp.bfloat16),
            pltpu.VMEM((hb, group, tile_rows, HEAD_DIM), jnp.float32),
            pltpu.VMEM((hb, group, tile_rows, 2 * HEAD_DIM), jnp.float32),
            dma((planes, kv_heads)),
            dma((kv_heads,)),
            dma((planes + 1,)),
            dma((kv_heads,)),
            dma((kv_heads,)),
            dma((kv_heads,)),
            dma((kv_heads,)),
        ],
        compiler_params=pltpu.CompilerParams(collective_id=0, has_side_effects=True),
    )(queries, key_rows, value_rows, tile_segment)


def solution(mesh):
    return jax.shard_map(
        local,
        mesh=mesh,
        in_specs=(
            P("blk", "ulysses", None),
            P("blk", "ulysses", None),
            P("blk", "ulysses", None),
            P(),
        ),
        out_specs=P("blk", "ulysses", None),
        check_vma=False,
    )
```

time: 138 us -> 53 us (0.38)
  the two profiles are of different devices: /device:TPU:5 before, /device:TPU:1 now
where the time goes in v1:
time: 53 us; the launch traced here: 52.9 us
  Pallas kernels  51 us (96%)
  local copies, waits for them, and re-layouts  1.87 us (4%)
    pallas_call x1, Pallas kernels, local(): pl.pallas_call(functools.partial(kernel, (ulysses, blocks, hx, hb)), out_...  51 us
    unnamed x1, local copies, waits for them, and re-layouts  1.87 us

profile of v1, /device:TPU:1, one launch (start us, length us, event | category | flops | bytes accessed | tf_op | source)
XLA Modules:
  0.0 52.9 jit_solution(2268531727429687592)
XLA Ops:
  0.0 51.0 %shard_map.46 = bf16[1,64,4096]{2,1,0:T(8,128)(2,1)} custom-call(bf16[1,64,4096]{2,1,0:T(8,128)(2,1)} %q_ref.1, bf16[1,64,1024]{2,1,0:T(8,128)(2,1)} %k_ref.1, bf16[1,64,1024]{2,1,0:T(8,128)(2,1)} %v_ref.1, s32[16]{0:T(128)} %seg_ref.1), custom_call_target="tpu_custom_call" | custom-call | tf_op jit(solution)/shard_map/pallas_call | solution.py:267
  51.0 1.9 %copy.6 = bf16[1,64,4096]{2,1,0:T(8,128)(2,1)} copy(bf16[1,64,4096]{2,1,0:T(8,128)(2,1)} %shard_map.46) | data formatting | bytes 1048576

commit v2 on v1

--- a/solution.py
+++ b/solution.py
@@ -16,7 +16,7 @@
 
 def kernel(
     dims, q_ref, k_ref, v_ref, seg_ref, out_ref,
-    kv, qb, ob, m_ref, acc_ref,
+    kv, qb, qs, ob, m_ref, acc_ref,
     kv_recv, kv_send, chain_send, q_recv, q_send, o_recv, o_send,
 ):
     ulysses, blocks, hx, hb = dims
@@ -127,6 +127,11 @@
     for j in range(1, peers):
         p = (me + peers - j) % peers
         arrived(qb.at[p], q_recv.at[p])
+
+    for p in range(peers):
+        for head in range(group):
+            low = head * tile_rows + (p % hx) * rows
+            qs[p // hx, low:low + rows, :] = qb[p, :, head * HEAD_DIM:(head + 1) * HEAD_DIM]
 
     def first_position(plane, bb):
         return (plane // gu_n * hb + bb) * block_len + (plane % gu_n) * tile_rows
@@ -148,35 +153,26 @@
             same = jnp.logical_and(key_seg == query_seg, query_seg % 2 == 1)
             limit = jnp.where(same, jnp.int32(2 ** 30), query_first - key_first)
             visible.append(delta <= limit)
-        for head in range(group):
-            query = qb[pl.ds(bb * hx, hx), :, head * HEAD_DIM:(head + 1) * HEAD_DIM]
-            query = query.reshape(tile_rows, HEAD_DIM)
-            scores = lax.dot_general(
-                query, keys, (((1,), (1,)), ((), ())), preferred_element_type=jnp.float32
-            )
-            scores = jnp.concatenate(
-                [
-                    jnp.where(visible[kb], scores[:, kb * tile_rows:(kb + 1) * tile_rows], MASKED)
-                    for kb in range(hb)
-                ],
-                axis=1,
-            )
-            old = m_ref[bb, head]
-            new = jnp.maximum(old, jnp.max(scores, axis=1, keepdims=True))
-            m_ref[bb, head] = new
-            factor = jnp.exp2((old - new) * scale)
-            weights = jnp.exp2((scores - new[:, :1]) * scale).astype(jnp.bfloat16)
-            product = jnp.dot(weights, values, preferred_element_type=jnp.float32)
-            acc_ref[bb, head] = (
-                jnp.concatenate([factor, factor], axis=1) * acc_ref[bb, head] + product
-            )
+        bound = jnp.where(jnp.concatenate(visible, axis=1), -MASKED, MASKED)
+        scores = lax.dot_general(
+            qs[bb], keys, (((1,), (1,)), ((), ())), preferred_element_type=jnp.float32
+        )
+        scores = jnp.minimum(scores, jnp.concatenate([bound] * group, axis=0))
+        old = m_ref[bb]
+        new = jnp.maximum(old, jnp.max(scores, axis=1, keepdims=True))
+        m_ref[bb] = new
+        factor = jnp.exp2((old - new) * scale)
+        top = jnp.concatenate([new] * (scores.shape[1] // HEAD_DIM), axis=1)
+        weights = jnp.exp2((scores - top) * scale).astype(jnp.bfloat16)
+        product = jnp.dot(weights, values, preferred_element_type=jnp.float32)
+        acc_ref[bb] = jnp.concatenate([factor, factor], axis=1) * acc_ref[bb] + product
 
     def attend_all(slot):
         def one(bb, carry):
             attend(slot, bb)
             return carry
 
-        lax.fori_loop(0, hb, one, 0)
+        lax.fori_loop(0, hb, one, 0, unroll=True)
 
     attend_all(g)
 
@@ -203,7 +199,7 @@
 
     for bb in range(hb):
         for head in range(group):
-            total = acc_ref[bb, head]
+            total = acc_ref[bb, head * tile_rows:(head + 1) * tile_rows]
             ob[bb * hx:(bb + 1) * hx, :, head * HEAD_DIM:(head + 1) * HEAD_DIM] = (
                 (total[:, :HEAD_DIM] / total[:, HEAD_DIM:])
                 .astype(jnp.bfloat16)
@@ -272,9 +268,10 @@
         scratch_shapes=[
             pltpu.VMEM((planes, kv_heads, 2, rows, HEAD_DIM), jnp.bfloat16),
             pltpu.VMEM((kv_heads, rows, group * HEAD_DIM), jnp.bfloat16),
+            pltpu.VMEM((hb, group * tile_rows, HEAD_DIM), jnp.bfloat16),
             pltpu.VMEM((kv_heads, rows, group * HEAD_DIM), jnp.bfloat16),
-            pltpu.VMEM((hb, group, tile_rows, HEAD_DIM), jnp.float32),
-            pltpu.VMEM((hb, group, tile_rows, 2 * HEAD_DIM), jnp.float32),
+            pltpu.VMEM((hb, group * tile_rows, HEAD_DIM), jnp.float32),
+            pltpu.VMEM((hb, group * tile_rows, 2 * HEAD_DIM), jnp.float32),
             dma((planes, kv_heads)),
             dma((kv_heads,)),
             dma((planes + 1,)),

time: 53 us -> 44.9 us (0.85)
  Pallas kernels: 51 us -> 42.8 us
    pallas_call x1, Pallas kernels: 51 us -> 42.8 us  [local(): pl.pallas_call(functools.partial(kernel, (ulysses, blocks, hx, hb)), out_...]
where the time goes in v2:
time: 44.9 us; the launch traced here: 44.7 us
  Pallas kernels  42.8 us (95%)
  local copies, waits for them, and re-layouts  1.87 us (4%)
    pallas_call x1, Pallas kernels, local(): pl.pallas_call(functools.partial(kernel, (ulysses, blocks, hx, hb)), out_...  42.8 us
    unnamed x1, local copies, waits for them, and re-layouts  1.87 us

profile of v2, /device:TPU:1, one launch (start us, length us, event | category | flops | bytes accessed | tf_op | source)
XLA Modules:
  0.0 44.7 jit_solution(638038688648422178)
XLA Ops:
  0.0 42.8 %shard_map.46 = bf16[1,64,4096]{2,1,0:T(8,128)(2,1)} custom-call(bf16[1,64,4096]{2,1,0:T(8,128)(2,1)} %q_ref.1, bf16[1,64,1024]{2,1,0:T(8,128)(2,1)} %k_ref.1, bf16[1,64,1024]{2,1,0:T(8,128)(2,1)} %v_ref.1, s32[16]{0:T(128)} %seg_ref.1), custom_call_target="tpu_custom_call" | custom-call | tf_op jit(solution)/shard_map/pallas_call | solution.py:263
  42.9 1.9 %copy.6 = bf16[1,64,4096]{2,1,0:T(8,128)(2,1)} copy(bf16[1,64,4096]{2,1,0:T(8,128)(2,1)} %shard_map.46) | data formatting | bytes 1048576

commit v3 on v2

--- a/solution.py
+++ b/solution.py
@@ -15,9 +15,9 @@
 
 
 def kernel(
-    dims, q_ref, k_ref, v_ref, seg_ref, out_ref,
-    kv, qb, qs, ob, m_ref, acc_ref,
-    kv_recv, kv_send, chain_send, q_recv, q_send, o_recv, o_send,
+    dims, q_hbm, k_hbm, v_hbm, seg_ref, out_ref,
+    q_ref, k_ref, v_ref, kv, qb, qs, ob, m_ref, acc_ref,
+    in_sems, kv_recv, kv_send, chain_send, q_recv, q_send, o_recv, o_send,
 ):
     ulysses, blocks, hx, hb = dims
     peers = hx * hb
@@ -41,6 +41,13 @@
     def plane_id(other):
         return ((other % gu_n) * hx + u % hx, (other // gu_n) * hb + b % hb)
 
+    loads = [
+        pltpu.make_async_copy(source, held, in_sems.at[i])
+        for i, (source, held) in enumerate(((k_hbm, k_ref), (v_hbm, v_ref), (q_hbm, q_ref)))
+    ]
+    for load in loads:
+        load.start()
+
     barrier = pltpu.get_barrier_semaphore()
     for j in range(1, peers):
         pl.semaphore_signal(
@@ -54,6 +61,11 @@
     @pl.when(g < planes - 1)
     def _():
         pl.semaphore_signal(barrier, inc=1, device_id=plane_id(g + 1), device_id_type=MESH)
+
+    m_ref[...] = jnp.full_like(m_ref, MASKED)
+    acc_ref[...] = jnp.zeros_like(acc_ref)
+    loads[0].wait()
+    loads[1].wait()
 
     ends = jnp.where(g > 0, 1, 0) + jnp.where(g < planes - 1, 1, 0)
     pl.semaphore_wait(barrier, peers - 1 + ends)
@@ -96,6 +108,7 @@
     def _():
         pass_own(g + 1, chain_send.at[g])
 
+    loads[2].wait()
     for j in range(1, peers):
         p = (me + j) % peers
         remote(
@@ -106,8 +119,6 @@
     kv[g, me, 0] = k_ref[0, :, columns(me, HEAD_DIM)]
     kv[g, me, 1] = v_ref[0, :, columns(me, HEAD_DIM)]
     qb[me] = q_ref[0, :, columns(me, width)]
-    m_ref[...] = jnp.full_like(m_ref, MASKED)
-    acc_ref[...] = jnp.zeros_like(acc_ref)
 
     def arrived(ref, sem):
         pltpu.make_async_copy(ref, ref, sem).wait()
@@ -123,6 +134,29 @@
         @pl.when(g < planes - 1)
         def _():
             pass_on(g, p, g + 1, chain_send.at[g])
+
+    near = jnp.minimum(g, planes - 1 - g)
+    inner = jnp.logical_and(g > 0, g < planes - 1)
+
+    def place(t):
+        both = t <= 2 * near
+        distance = jnp.where(both, (t + 1) // 2, t - near)
+        below = jnp.where(both, t % 2 == 1, g > planes - 1 - g)
+        return jnp.where(below, g - distance, g + distance), jnp.where(below, g + 1, g - 1)
+
+    def take(t, half, when):
+        @pl.when(when)
+        def _():
+            slot, target = place(t)
+            for p in range(half * peers // 2, (half + 1) * peers // 2):
+                arrived(kv.at[slot, p], kv_recv.at[slot, p])
+
+                @pl.when(inner)
+                def _():
+                    pass_on(slot, p, target, chain_send.at[slot])
+
+    for half in range(2):
+        take(jnp.int32(1), half, planes > 1)
 
     for j in range(1, peers):
         p = (me + peers - j) % peers
@@ -140,14 +174,14 @@
         jnp.int32, (tile_rows, tile_rows), 0
     )
 
-    def attend(slot, bb):
+    def attend(slot, bb, low, high):
         query_first = first_position(g, bb)
         query_seg = seg_ref[query_first // TILE]
-        keys = kv[slot, :, 0].reshape(hb * tile_rows, HEAD_DIM)
-        values = kv[slot, :, 1].reshape(hb * tile_rows, HEAD_DIM)
+        keys = kv[slot, low * hx:high * hx, 0].reshape(-1, HEAD_DIM)
+        values = kv[slot, low * hx:high * hx, 1].reshape(-1, HEAD_DIM)
         values = jnp.concatenate([values, jnp.ones_like(values)], axis=1)
         visible = []
-        for kb in range(hb):
+        for kb in range(low, high):
             key_first = first_position(slot, kb)
             key_seg = seg_ref[key_first // TILE]
             same = jnp.logical_and(key_seg == query_seg, query_seg % 2 == 1)
@@ -167,37 +201,28 @@
         product = jnp.dot(weights, values, preferred_element_type=jnp.float32)
         acc_ref[bb] = jnp.concatenate([factor, factor], axis=1) * acc_ref[bb] + product
 
-    def attend_all(slot):
-        def one(bb, carry):
-            attend(slot, bb)
-            return carry
-
-        lax.fori_loop(0, hb, one, 0, unroll=True)
-
-    attend_all(g)
-
-    near = jnp.minimum(g, planes - 1 - g)
-
     def step(t, carry):
-        both = t <= 2 * near
-        distance = jnp.where(both, (t + 1) // 2, t - near)
-        below = jnp.where(both, t % 2 == 1, g > planes - 1 - g)
-        slot = jnp.where(below, g - distance, g + distance)
-        target = jnp.where(below, g + 1, g - 1)
-        onward = jnp.logical_and(target >= 0, target < planes)
-        for p in range(peers):
-            arrived(kv.at[slot, p], kv_recv.at[slot, p])
-
-            @pl.when(onward)
-            def _():
-                pass_on(slot, p, target, chain_send.at[slot])
-
-        attend_all(slot)
+        for half in range(2):
+            take(t, half, jnp.logical_and(t > 1, jnp.logical_not(inner)))
+        later = jnp.logical_and(t + 2 < planes, inner)
+        take(t + 2, 0, later)
+        slot = jnp.where(t == 0, g, place(t)[0])
+        for bb in range(hb):
+            attend(slot, bb, 0, hb)
+        take(t + 2, 1, later)
         return carry
 
-    lax.fori_loop(1, planes, step, 0)
-
+    lax.fori_loop(0, planes - 1, step, 0)
+
+    last = planes - 1
+    wait_last = jnp.logical_and(last > 1, jnp.logical_not(inner))
+    slot = place(last)[0]
+    take(last, 0, wait_last)
     for bb in range(hb):
+        attend(slot, bb, 0, hb // 2)
+    take(last, 1, wait_last)
+
+    def finish(bb):
         for head in range(group):
             total = acc_ref[bb, head * tile_rows:(head + 1) * tile_rows]
             ob[bb * hx:(bb + 1) * hx, :, head * HEAD_DIM:(head + 1) * HEAD_DIM] = (
@@ -205,6 +230,8 @@
                 .astype(jnp.bfloat16)
                 .reshape(hx, rows, HEAD_DIM)
             )
+
+    def give(bb):
         for ux in range(hx):
             p = bb * hx + ux
 
@@ -214,6 +241,16 @@
                     ob.at[p], out_ref.at[0, :, columns(me, width)],
                     o_send.at[p], o_recv.at[me], peer_id(p),
                 ).start()
+
+    spread = max(1, hb // 2)
+    for first in range(spread):
+        share = range(first, hb, spread)
+        for bb in share:
+            attend(slot, bb, hb // 2, hb)
+        for bb in share:
+            finish(bb)
+        for bb in share:
+            give(bb)
 
     out_ref[0, :, columns(me, width)] = ob[me]
     for j in range(1, peers):
@@ -257,21 +294,26 @@
     planes = ulysses * blocks // kv_heads
     group = queries.shape[2] // HEAD_DIM // kv_heads
     tile_rows = hx * rows
-    assert ulysses % hx == 0 and TILE % tile_rows == 0
+    assert ulysses % hx == 0 and planes > 1 and hb % 2 == 0 and TILE % tile_rows == 0
     vmem = pl.BlockSpec(memory_space=pltpu.VMEM)
+    hbm = pl.BlockSpec(memory_space=pl.ANY)
     dma = pltpu.SemaphoreType.DMA
     return pl.pallas_call(
         functools.partial(kernel, (ulysses, blocks, hx, hb)),
-        out_shape=jax.ShapeDtypeStruct(queries.shape, jnp.bfloat16),
-        in_specs=[vmem, vmem, vmem, pl.BlockSpec(memory_space=pltpu.SMEM)],
+        out_shape=pltpu.VMEM(queries.shape, jnp.bfloat16),
+        in_specs=[hbm, hbm, hbm, pl.BlockSpec(memory_space=pltpu.SMEM)],
         out_specs=vmem,
         scratch_shapes=[
+            pltpu.VMEM(queries.shape, jnp.bfloat16),
+            pltpu.VMEM(key_rows.shape, jnp.bfloat16),
+            pltpu.VMEM(value_rows.shape, jnp.bfloat16),
             pltpu.VMEM((planes, kv_heads, 2, rows, HEAD_DIM), jnp.bfloat16),
             pltpu.VMEM((kv_heads, rows, group * HEAD_DIM), jnp.bfloat16),
             pltpu.VMEM((hb, group * tile_rows, HEAD_DIM), jnp.bfloat16),
             pltpu.VMEM((kv_heads, rows, group * HEAD_DIM), jnp.bfloat16),
             pltpu.VMEM((hb, group * tile_rows, HEAD_DIM), jnp.float32),
             pltpu.VMEM((hb, group * tile_rows, 2 * HEAD_DIM), jnp.float32),
+            dma((3,)),
             dma((planes, kv_heads)),
             dma((kv_heads,)),
             dma((planes + 1,)),

time: 44.9 us -> 38.1 us (0.85)
  Pallas kernels: 42.8 us -> 37.1 us
  local copies, waits for them, and re-layouts: 1.87 us -> 0.8 us
    pallas_call x1, Pallas kernels: 42.8 us -> 37.1 us  [local(): pl.pallas_call(functools.partial(kernel, (ulysses, blocks, hx, hb)), out_...]
    unnamed x1, local copies, waits for them, and re-layouts: 1.87 us -> 0.8 us
where the time goes in v3:
time: 38.1 us; the launch traced here: 38 us
  Pallas kernels  37.1 us (97%)
  local copies, waits for them, and re-layouts  0.8 us (2%)
    pallas_call x1, Pallas kernels, local(): pl.pallas_call(functools.partial(kernel, (ulysses, blocks, hx, hb)), out_...  37.1 us
    unnamed x1, local copies, waits for them, and re-layouts  0.8 us

profile of v3, /device:TPU:1, one launch (start us, length us, event | category | flops | bytes accessed | tf_op | source)
XLA Modules:
  0.0 38.0 jit_solution(12934193997486933695)
XLA Ops:
  0.0 37.1 %shard_map.46 = bf16[1,64,4096]{2,1,0:T(8,128)(2,1)S(1)} custom-call(bf16[1,64,4096]{2,1,0:T(8,128)(2,1)} %q_hbm.1, bf16[1,64,1024]{2,1,0:T(8,128)(2,1)} %k_hbm.1, bf16[1,64,1024]{2,1,0:T(8,128)(2,1)} %v_hbm.1, s32[16]{0:T(128)} %seg_ref.1), custom_call_target="tpu_custom_call" | custom-call | tf_op jit(solution)/shard_map/pallas_call | solution.py:301
  37.2 0.8 %copy.6 = bf16[1,64,4096]{2,1,0:T(8,128)(2,1)} copy(bf16[1,64,4096]{2,1,0:T(8,128)(2,1)S(1)} %shard_map.46) | data formatting | bytes 1048576
